TPU v7x, 32 devices: a whole 2x2x4 slice. The times are simulated.
32 devices in a mesh: cls: 4 (over y, x), org: 8 (over z, core).
Axes of the slice: x: 2, y: 2, z: 4, core: 2. Of those that a mesh axis runs over, the one named last changes fastest.
Arguments:
- flows_start: float32 [8, 49152], P('cls', 'org'), may hold values from 150 to 300
- interaction: float32 [8, 8, 49152], P('cls', None, 'org'), may hold values from 0.2 to 2
- free_time: float32 [8, 49152], P('cls', 'org'), may hold values from 0.01 to 0.1
- capacity: float32 [49152], P('org'), may hold values from 300 to 900
- demand: int32 [8, 8, 60], P('cls', 'org'), may hold values from 0 to 15
- incidence: int32 [2, 8, 8, 2, 49152], P(None, 'cls', 'org'), may hold values from 0 to 1073741823, as said below
- step_size: float32 [2], replicated, may hold values from 0.3 to 0.6
Outputs:
- flows: float32 [8, 49152], P('cls', 'org')
- costs: float32 [8, 49152], P('cls', 'org')
- skims: float32 [2, 8, 8, 60], P(None, 'cls', 'org')
- gaps: float32 [2], replicated
Inputs may be any that keep to these rules, and one draw needn't show every extreme that they name: Bit b of incidence[k, c, o, w, l] tells whether link l lies on class c's path from anchor o to destination w * 30 + b in iteration k; each path is the union of 4 runs of 64 consecutive links (counted cyclically over the links) at drawn starts, the first of which is shared by all 30 destinations of one word.
All inputs are finite; a program needn't handle non-finite values.
Results may differ from a plain program's by a relative error of at most 0.0013.
Values sent between devices are 32-bit elements; how exact they have to be, the bound alone decides.
A program may use at most 256 MiB of HBM per device.

v0:
```python
import jax
import jax.numpy as jnp
from jax import lax
from jax.sharding import PartitionSpec as P

BITS = 30
ITERS = 2
HIGH = lax.Precision.HIGHEST


def unpack_half(packed):
    shifts = jnp.arange(BITS, dtype=jnp.int32)
    bit_table = jnp.bitwise_and(jnp.right_shift(packed[..., :, None, :], shifts[:, None]), 1)
    new_shape = packed.shape[:-2] + (packed.shape[-2] * BITS, packed.shape[-1])
    return bit_table.reshape(new_shape).astype(jnp.bfloat16)


def link_cost(flows_all, inter, free, cap):
    load_sum = jnp.einsum("cel,el->cl", inter, flows_all, precision=HIGH)
    load_ratio = load_sum / cap
    square = load_ratio * load_ratio
    return free * (1.0 + 0.15 * square * square)


def split_three(values):
    upper = values.astype(jnp.bfloat16)
    remain = values - upper.astype(jnp.float32)
    middle = remain.astype(jnp.bfloat16)
    lowest = (remain - middle.astype(jnp.float32)).astype(jnp.bfloat16)
    return jnp.stack([upper, middle, lowest], axis=1)


def skim_block(bit_table, cost_block):
    parts = split_three(cost_block)
    terms = jnp.einsum("codl,cpl->cpod", bit_table, parts, preferred_element_type=jnp.float32)
    return jnp.sum(terms, axis=1)


def anchor_loads_local(packed_all, trips_half, link_shard, block_count):

    def one_block(block_index):
        word_block = lax.dynamic_slice_in_dim(packed_all, block_index * link_shard, link_shard, 3)
        bit_table = unpack_half(word_block)
        return jnp.einsum("cod,codl->cl", trips_half, bit_table, preferred_element_type=jnp.float32)

    blocks = lax.map(one_block, jnp.arange(block_count, dtype=jnp.int32))
    return jnp.moveaxis(blocks, 0, 1).reshape(blocks.shape[1], block_count * link_shard)


def make_fold(packed_all, link_shard):

    def fold_links(skim_carry, portion, first):
        turn_count = portion.shape[1] // link_shard

        def advance(skim_sum, block_index):
            offset = block_index * link_shard
            word_block = lax.dynamic_slice_in_dim(packed_all, offset, link_shard, 3)
            bit_table = unpack_half(word_block)
            cost_block = lax.dynamic_slice_in_dim(portion, offset, link_shard, 1)
            return (skim_sum + skim_block(bit_table, cost_block), None)

        result, unused = lax.scan(advance, skim_carry, jnp.arange(turn_count, dtype=jnp.int32))
        return result

    return fold_links


def both_totals(cost_part, path_part):
    return lax.psum((cost_part, path_part), ("cls", "org"))


def shards(flows_start, interaction, free_time, capacity, demand, incidence, step_size):
    org_count = lax.axis_size("org")
    link_shard = flows_start.shape[1]
    dest_count = demand.shape[2]
    class_local = demand.shape[0]
    demand_real = demand.astype(jnp.float32)
    trips_half = demand.astype(jnp.bfloat16)
    own_start = lax.axis_index("org") * link_shard
    skim_init = jnp.zeros((class_local, demand.shape[1], dest_count), jnp.float32)
    skim_list = []
    gap_list = []
    inter_full, free_full, cap_full, flow_now = (
        lax.all_gather(interaction, "org", axis=2, tiled=True),
        lax.all_gather(free_time, "org", axis=1, tiled=True),
        lax.all_gather(capacity, "org", axis=0, tiled=True),
        lax.all_gather(flows_start, "org", axis=1, tiled=True),
    )

    def full_cost(flow_value):
        flows_all = lax.all_gather(flow_value, "cls", axis=0, tiled=True)
        return link_cost(flows_all, inter_full, free_full, cap_full)

    for iteration in range(ITERS):
        cost_now = full_cost(flow_now)
        fold_links = make_fold(incidence[iteration], link_shard)
        skim_now = fold_links(skim_init, cost_now, jnp.int32(0))
        partial_value = anchor_loads_local(incidence[iteration], trips_half, link_shard, org_count)
        aon = lax.psum(partial_value, "org")
        product = lax.dynamic_slice_in_dim(cost_now * flow_now, own_start, link_shard, 1)
        cost_total, path_total = both_totals(jnp.sum(product), jnp.sum(demand_real * skim_now))
        gap_list.append((cost_total - path_total) / cost_total)
        skim_list.append(skim_now)
        flow_now = flow_now + step_size[iteration] * (aon - flow_now)
    cost_final = full_cost(flow_now)
    flow_out = lax.dynamic_slice_in_dim(flow_now, own_start, link_shard, 1)
    cost_out = lax.dynamic_slice_in_dim(cost_final, own_start, link_shard, 1)
    return (flow_out, cost_out, jnp.stack(skim_list), jnp.stack(gap_list))


def solution(mesh):
    placed = (
        P("cls", "org"),
        P("cls", None, "org"),
        P("cls", "org"),
        P("org"),
        P("cls", "org", None),
        P(None, "cls", "org", None, None),
        P(),
    )
    return jax.shard_map(
        shards,
        mesh=mesh,
        in_specs=placed,
        out_specs=(P("cls", "org"), P("cls", "org"), P(None, "cls", "org", None), P()),
        check_vma=False,
    )
```

profile of v0, /device:TPU:0, one launch (start us, length us, event | category | flops | bytes accessed | tf_op | source)
XLA Modules:
  0.0 387.4 jit_solution(10713880894416797273)
XLA Ops:
  10.9 32.3 %while.43 = (s32[]{:T(128)}, f32[8,2,6144]{2,1,0:T(2,128)S(1)}, s32[8]{0:T(128)S(1)}, s32[2,1,2,49152]{3,0,2,1:T(2,128)S(1)}, bf16[2,1,60]{2,0,1:T(2,128)(2,1)S(...) while((s32[]{:T(128)}, f32[8,2,6144]{2,1,0:T(2,128)S(1)}, s32[8]{0:T(128)S(1)}, ...), condition=%wide.region_4.5_spmd, body=%wide.region_3.4_spmd.sunk | while | flops 3686406 | bytes 3392847 | solution.py:46
  12.3 1.7 fusion.83
  16.3 1.7 fusion.83
  20.3 1.7 fusion.83
  24.4 1.7 fusion.83
  28.4 1.7 fusion.83
  32.5 1.7 fusion.83
  36.5 1.7 fusion.83
  40.5 1.7 fusion.83
  44.3 32.3 %while.42 = (s32[]{:T(128)}, f32[8,2,6144]{2,1,0:T(2,128)S(1)}, s32[8]{0:T(128)S(1)}, s32[2,1,2,49152]{3,0,2,1:T(2,128)S(1)}, bf16[2,1,60]{2,0,1:T(2,128)(2,1)S(...) while((s32[]{:T(128)}, f32[8,2,6144]{2,1,0:T(2,128)S(1)}, s32[8]{0:T(128)S(1)}, ...), condition=%wide.region_1.0_spmd, body=%wide.region_0.1_spmd.sunk | while | flops 3686406 | bytes 3392847 | solution.py:46
  45.7 1.7 fusion.79
  49.7 1.7 fusion.79
  53.8 1.7 fusion.79
  57.8 1.7 fusion.79
  61.8 1.7 fusion.79
  65.9 1.7 fusion.79
  69.9 1.7 fusion.79
  74.0 1.7 fusion.79
  77.5 17.5 %all_gather.21 = f32[2,49152]{1,0:T(2,128)} all-gather(f32[2,6144]{1,0:T(2,128)S(1)} %copy-done.7), channel_id=1, replica_groups=mesh['cls'=4,'org'=8] {'org'}, dimensions={1}, use_global_device_ids=true | all-gather | bytes 442368 | tf_op jit(solution)/shard_map/all_gather | solution.py:87
  95.7 42.7 %all-reduce.4.cloned.1.call-done = (f32[2,49152]{1,0:T(2,128)}, f32[2,49152]{1,0:T(2,128)}) async-done(((f32[2,49152]{1,0:T(2,128)}, f32[2,49152]{1,0:T(2,128)}), (f32[2,49152]{1,0:T(2,128)}, f32[2,49152]{1,0:T(2,128)})) %all-reduce.4.cloned.1.call-update) | async-done | bytes 786448 | tf_op jit(solution)/shard_map/psum | solution.py:99
  138.4 3.8 multiply_add_fusion
  143.5 15.2 %all_gather.25 = f32[49152]{0:T(1024)} all-gather(f32[6144]{0:T(1024)S(1)} %copy-done.9), channel_id=1, replica_groups=mesh['cls'=4,'org'=8] {'org'}, dimensions={0}, use_global_device_ids=true | all-gather | bytes 221184 | tf_op jit(solution)/shard_map/all_gather | solution.py:86
  158.7 14.7 %all_gather.22 = f32[2,49152]{1,0:T(2,128)S(1)} all-gather(f32[2,6144]{1,0:T(2,128)S(1)} %copy-done.8), channel_id=1, replica_groups=mesh['cls'=4,'org'=8] {'org'}, dimensions={1}, use_global_device_ids=true | all-gather | bytes 442368 | tf_op jit(solution)/shard_map/all_gather | solution.py:85
  174.8 2.5 reshape.94
  177.3 2.5 reshape.92
  179.8 24.8 %all-gather.14.cloned.1.call-done = f32[4,2,49152]{2,1,0:T(2,128)} async-done(((f32[1,2,49152]{2,1,0:T(2,128)}), f32[4,2,49152]{2,1,0:T(2,128)}) %all-gather.14.cloned.1.call-update) | async-done | bytes 1572880 | tf_op jit(solution)/shard_map/all_gather | solution.py:91
  204.6 3.6 reshape.96
  208.2 36.0 %all-gather.8.cloned.1.call-done = f32[2,8,49152]{2,1,0:T(8,128)} async-done(((f32[2,8,6144]{2,1,0:T(8,128)}), f32[2,8,49152]{2,1,0:T(8,128)}) %all-gather.8.cloned.1.call-update) | async-done | bytes 3145744 | tf_op jit(solution)/shard_map/all_gather | solution.py:84
  244.2 6.9 %multiply_reduce_fusion.1 = (f32[49152,2]{0,1:T(2,128)S(1)}, f32[49152,2]{0,1:T(2,128)S(1)}, f32[49152,2]{0,1:T(2,128)}) fusion(f32[2,8,49152]{2,1,0:T(8,128)} %all-gather.8.cloned.1.call-done, f32[49152,8]{0,1:T(8,128)S(1)} %bitcast.155, f32[49152,8]{0,1:T(8,128)} %bitcast.157, f32[49152,8]{0,1:T(8,128)S(1)} %bitcast.156), kind=kLoop, calls=%fused_computation.59 | loop fusion | flops 4423680 | bytes 9043968 | tf_op jit(solution)/shard_map/cel,el->cl/dot_general | solution.py:19
  253.4 39.4 %while.44 = (s32[]{:T(128)}, f32[2,1,60]{2,0,1:T(2,128)S(1)}, s32[8]{0:T(128)S(1)}, f32[2,49152]{1,0:T(2,128)S(1)}, s32[2,1,2,49152]{3,0,2,1:T(2,128)}, /*index=5*/s32[]{:T(128)}, s32[1]{0:T(128)}, s32[]{:T(128)}, s32[]{:T(128)}) while((s32[]{:T(128)}, f32[2,1,60]{2,0,1:T(2,128)S(1)}, s32[8]{0:T(128)S(1)}, ...), condition=%wide.region_8.9_spmd.clone, body=%wide.region_6.8_spmd.clone.sunk | while | flops 6943207 | bytes 3615725 | solution.py:62
  255.9 1.7 fusion.87
  260.8 1.7 fusion.87
  265.7 1.7 fusion.87
  270.6 1.7 fusion.87
  275.5 1.7 fusion.87
  280.5 1.7 fusion.87
  285.4 1.7 fusion.87
  290.3 1.7 fusion.87
  294.2 39.4 %while.45 = (s32[]{:T(128)}, f32[2,1,60]{2,0,1:T(2,128)S(1)}, s32[8]{0:T(128)S(1)}, f32[2,49152]{1,0:T(2,128)S(1)}, s32[2,1,2,49152]{3,0,2,1:T(2,128)}, /*index=5*/s32[]{:T(128)}, s32[1]{0:T(128)}, s32[]{:T(128)}, s32[]{:T(128)}) while((s32[]{:T(128)}, f32[2,1,60]{2,0,1:T(2,128)S(1)}, s32[8]{0:T(128)S(1)}, ...), condition=%wide.region_11.12_spmd.clone, body=%wide.region_9.11_spmd.clone.sunk | while | flops 6943207 | bytes 3615725 | solution.py:62
  296.7 1.7 fusion.93
  301.6 1.7 fusion.93
  306.5 1.7 fusion.93
  311.5 1.7 fusion.93
  316.4 1.7 fusion.93
  321.3 1.7 fusion.93
  326.2 1.7 fusion.93
  331.1 1.7 fusion.93
  334.2 39.7 %all-reduce = (f32[]{:T(128)}, f32[]{:T(128)}, f32[]{:T(128)}, f32[]{:T(128)}) all-reduce(f32[]{:T(128)} %fusion.53, f32[]{:T(128)} %get-tuple-element.186, f32[]{:T(128)} %fusion.54, f32[]{:T(128)} %get-tuple-element.185), channel_id=1, replica_groups=mesh['cls'=4,'org'=8] {'cls','org'}, use_global_device_ids=true, to_apply=%region_17.18 | all-reduce | flops 4 | bytes 32 | tf_op jit(solution)/shard_map/psum | solution.py:69
  (329 shorter events, 79.8 us)
Async XLA Ops:
  8.0 130.4 %all-reduce.4.cloned.1.call-start = ((), (), s32[]{:S(2)}) async-start(), calls=%async_computation.4 | async-start | bytes 1572864 | tf_op jit(solution)/shard_map/psum | solution.py:99
  8.0 1.5 copy-start.11
  43.2 1.0 copy-start
  43.2 1.1 copy-start.6
  43.3 34.1 %copy-start.7 = (f32[2,6144]{1,0:T(2,128)S(1)}, f32[2,6144]{1,0:T(2,128)}, u32[]{:S(2)}) copy-start(f32[2,6144]{1,0:T(2,128)} %param.15) | copy-start | bytes 147460
  76.6 0.8 copy-start.5
  76.6 65.5 %copy-start.1 = (s32[2,1,2,49152]{3,0,2,1:T(2,128)}, s32[2,1,2,49152]{3,0,2,1:T(2,128)S(1)}, u32[]{:S(2)}) copy-start(s32[2,1,2,49152]{3,0,2,1:T(2,128)S(1)} %get-tuple-element.496) | copy-start | bytes 2359300
  76.6 18.4 %copy-start.10 = (f32[2]{0:T(128)S(1)}, f32[2]{0:T(128)}, u32[]{:S(2)}) copy-start(f32[2]{0:T(128)} %param.21) | copy-start | bytes 28
  77.4 97.4 %all-gather.12.cloned.1.call-start = ((), (), s32[]{:S(2)}) async-start(), calls=%async_computation.2 | async-start | bytes 1966080 | tf_op jit(solution)/shard_map/all_gather | solution.py:91
  95.0 82.3 %all-gather.10.cloned.1.call-start = ((), (), s32[]{:S(2)}) async-start(), calls=%async_computation.1 | async-start | bytes 1966080 | tf_op jit(solution)/shard_map/all_gather | solution.py:91
  138.4 5.1 %copy-start.9 = (f32[6144]{0:T(1024)S(1)}, f32[6144]{0:T(1024)}, u32[]{:S(2)}) copy-start(f32[6144]{0:T(1024)} %param.18) | copy-start | bytes 73732
  138.4 20.3 %copy-start.8 = (f32[2,6144]{1,0:T(2,128)S(1)}, f32[2,6144]{1,0:T(2,128)}, u32[]{:S(2)}) copy-start(f32[2,6144]{1,0:T(2,128)} %param.17) | copy-start | bytes 147460
  142.2 62.4 %all-gather.14.cloned.1.call-start = ((), (), s32[]{:S(2)}) async-start(), calls=%async_computation.3 | async-start | bytes 1966080 | tf_op jit(solution)/shard_map/all_gather | solution.py:91
  142.8 101.5 %all-gather.8.cloned.1.call-start = ((), (), s32[]{:S(2)}) async-start(), calls=%async_computation | async-start | bytes 3538944 | tf_op jit(solution)/shard_map/all_gather | solution.py:84
  244.2 6.9 %copy-start.2 = (f32[49152]{0:T(1024)S(1)}, f32[49152]{0:T(1024)}, u32[]{:S(2)}) copy-start(f32[49152]{0:T(1024)} %all_gather.25) | copy-start | bytes 589828
  294.2 83.5 %copy-start.3 = (f32[49152]{0:T(1024)S(1)}, f32[49152]{0:T(1024)}, u32[]{:S(2)}) copy-start(f32[49152]{0:T(1024)} %all_gather.25) | copy-start | bytes 589828
  294.2 83.5 %copy-start.4 = (f32[49152,2]{0,1:T(2,128)S(1)}, f32[49152,2]{0,1:T(2,128)}, u32[]{:S(2)}) copy-start(f32[49152,2]{0,1:T(2,128)} %get-tuple-element.184) | copy-start | bytes 1179652
Sparse Core Ops, SparseCore 0:
  77.5 60.7 all-reduce.3
Sparse Core Ops, SparseCore 1:
  95.1 31.7 all-gather.11
  142.3 29.8 all-gather.9
  173.8 30.7 all-gather.13
  206.2 38.0 all-gather.7
where the time goes:
time: 389 us; the launch traced here: 387 us
  waiting for transfers between devices  105 us (27%)
  blocking collectives  87 us (22%)
  other arithmetic  73.1 us (19%)
  local copies, waits for them, and re-layouts  54.4 us (14%)
  matrix products  25.3 us (7%)
  loops' own time  22.7 us (6%)
  between operations  19.7 us (5%)
    convert_element_type x32, other arithmetic, unpack_half(): return bit_table.reshape(new_shape).astype(jnp.bfloat16)  55.2 us
    psum x1, waiting for transfers between devices, shards(): aon = lax.psum(partial_value, 'org')  42.7 us
    psum x1, blocking collectives, both_totals(): return lax.psum((cost_part, path_part), ('cls', 'org'))  39.7 us
    all_gather x1, waiting for transfers between devices, shards(): lax.all_gather(interaction, 'org', axis=2, tiled=True)  36 us
    all_gather x3, waiting for transfers between devices, full_cost(): flows_all = lax.all_gather(flow_value, 'cls', axis=0, tiled=True)  24.8 us
    dynamic_slice x32, local copies, waits for them, and re-layouts, fold_links(): lax.scan(advance, skim_carry, jnp.arange(turn_count, dtype=jnp.int32))  18.8 us
    all_gather x1, blocking collectives, shards(): lax.all_gather(flows_start, 'org', axis=1, tiled=True)  17.5 us
    shift_right_arithmetic x96, local copies, waits for them, and re-layouts, unpack_half(): jnp.right_shift(packed[..., :, None, :], shifts[:, None])  17.5 us
  transfers between devices with their start and end apart: 5, of which 3 were waited for; matrix products, arithmetic and copies ran while one was open for 4% of the time, Pallas kernels for 0%

commit v1 on v0

--- a/solution.py
+++ b/solution.py
@@ -96,7 +96,9 @@
         fold_links = make_fold(incidence[iteration], link_shard)
         skim_now = fold_links(skim_init, cost_now, jnp.int32(0))
         partial_value = anchor_loads_local(incidence[iteration], trips_half, link_shard, org_count)
-        aon = lax.psum(partial_value, "org")
+        aon = partial_value
+        for hop in (1, 2, 4):
+            aon = aon + lax.ppermute(aon, "org", [(dev, dev ^ hop) for dev in range(8)])
         product = lax.dynamic_slice_in_dim(cost_now * flow_now, own_start, link_shard, 1)
         cost_total, path_total = both_totals(jnp.sum(product), jnp.sum(demand_real * skim_now))
         gap_list.append((cost_total - path_total) / cost_total)

time: 389 us -> 415 us (1.067)
  blocking collectives: 87 us -> 102 us
  starting transfers between devices: 0.21 us -> 8.56 us
  waiting for transfers between devices: 105 us -> 110 us
    psum x1 -> x0, waiting for transfers between devices: 42.7 us -> none  [shards(): aon = lax.psum(partial_value, 'org')]
    all_gather x3, waiting for transfers between devices: 24.8 us -> 52.7 us  [full_cost(): flows_all = lax.all_gather(flow_value, 'cls', axis=0, tiled=True)]
    ppermute x0 -> x6, waiting for transfers between devices: none -> 20.2 us  [shards(): aon = aon + lax.ppermute(aon, 'org', [(dev, dev ^ hop) for dev in range(8)])]
    all_gather x1, blocking collectives: 17.5 us -> 32.9 us  [shards(): lax.all_gather(flows_start, 'org', axis=1, tiled=True)]
    ppermute x0 -> x6, starting transfers between devices: none -> 8.4 us  [shards(): aon = aon + lax.ppermute(aon, 'org', [(dev, dev ^ hop) for dev in range(8)])]
    unnamed x27 -> x23, local copies, waits for them, and re-layouts: 10.4 us -> 9.03 us
  transfers between devices with their start and end apart: 5 -> 10, of which waited for: 3 -> 5; matrix products, arithmetic and copies ran while one was open for 4% -> 10% of each run, Pallas kernels for 0% -> 0%
where the time goes in v1:
time: 415 us; the launch traced here: 414 us
  waiting for transfers between devices  110 us (27%)
  blocking collectives  102 us (25%)
  other arithmetic  73.9 us (18%)
  local copies, waits for them, and re-layouts  53.1 us (13%)
  matrix products  25.3 us (6%)
  loops' own time  22.7 us (5%)
  between operations  17.9 us (4%)
  starting transfers between devices  8.56 us (2%)
    convert_element_type x32, other arithmetic, unpack_half(): return bit_table.reshape(new_shape).astype(jnp.bfloat16)  55.2 us
    all_gather x3, waiting for transfers between devices, full_cost(): flows_all = lax.all_gather(flow_value, 'cls', axis=0, tiled=True)  52.7 us
    psum x1, blocking collectives, both_totals(): return lax.psum((cost_part, path_part), ('cls', 'org'))  39.6 us
    all_gather x1, waiting for transfers between devices, shards(): lax.all_gather(interaction, 'org', axis=2, tiled=True)  36.1 us
    all_gather x1, blocking collectives, shards(): lax.all_gather(flows_start, 'org', axis=1, tiled=True)  32.9 us
    ppermute x6, waiting for transfers between devices, shards(): aon = aon + lax.ppermute(aon, 'org', [(dev, dev ^ hop) for dev in range(8)])  20.2 us
    dynamic_slice x32, local copies, waits for them, and re-layouts, fold_links(): lax.scan(advance, skim_carry, jnp.arange(turn_count, dtype=jnp.int32))  18.8 us
    shift_right_arithmetic x96, local copies, waits for them, and re-layouts, unpack_half(): jnp.right_shift(packed[..., :, None, :], shifts[:, None])  17.5 us
  transfers between devices with their start and end apart: 10, of which 5 were waited for; matrix products, arithmetic and copies ran while one was open for 10% of the time, Pallas kernels for 0%

profile of v1, /device:TPU:0, one launch (start us, length us, event | category | flops | bytes accessed | tf_op | source)
XLA Modules:
  0.0 414.0 jit_solution(5425501579139453971)
XLA Ops:
  10.1 32.3 %while.42 = (s32[]{:T(128)}, f32[8,2,6144]{2,1,0:T(2,128)S(1)}, s32[8]{0:T(128)S(1)}, s32[2,1,2,49152]{3,0,2,1:T(2,128)S(1)}, bf16[2,1,60]{2,0,1:T(2,128)(2,1)S(...) while((s32[]{:T(128)}, f32[8,2,6144]{2,1,0:T(2,128)S(1)}, s32[8]{0:T(128)S(1)}, ...), condition=%wide.region_1.0_spmd, body=%wide.region_0.1_spmd.sunk | while | flops 3686406 | bytes 3392847 | solution.py:46
  11.4 1.7 fusion.79
  15.5 1.7 fusion.79
  19.5 1.7 fusion.79
  23.6 1.7 fusion.79
  27.6 1.7 fusion.79
  31.6 1.7 fusion.79
  35.7 1.7 fusion.79
  39.7 1.7 fusion.79
  43.4 32.3 %while.43 = (s32[]{:T(128)}, f32[8,2,6144]{2,1,0:T(2,128)S(1)}, s32[8]{0:T(128)S(1)}, s32[2,1,2,49152]{3,0,2,1:T(2,128)S(1)}, bf16[2,1,60]{2,0,1:T(2,128)(2,1)S(...) while((s32[]{:T(128)}, f32[8,2,6144]{2,1,0:T(2,128)S(1)}, s32[8]{0:T(128)S(1)}, ...), condition=%wide.region_3.4_spmd, body=%wide.region_2.3_spmd.sunk | while | flops 3686406 | bytes 3392847 | solution.py:46
  44.7 1.7 fusion.83
  48.7 1.7 fusion.83
  52.8 1.7 fusion.83
  56.8 1.7 fusion.83
  60.9 1.7 fusion.83
  64.9 1.7 fusion.83
  68.9 1.7 fusion.83
  73.0 1.7 fusion.83
  76.4 2.7 collective-permute-start.1
  80.8 8.3 %collective-permute-done.1 = f32[2,49152]{1,0:T(2,128)S(1)} collective-permute-done((f32[2,49152]{1,0:T(2,128)S(1)}, f32[2,49152]{1,0:T(2,128)S(1)}, u32[]{:S(2)}, u32[]{:S(2)}) %collective-permute-start.1) | collective-permute-done | bytes 393248 | tf_op jit(solution)/shard_map/ppermute | solution.py:101
  89.3 3.1 collective-permute-start.2
  92.4 11.9 %collective-permute-done.4 = f32[2,49152]{1,0:T(2,128)S(1)} collective-permute-done((f32[2,49152]{1,0:T(2,128)S(1)}, f32[2,49152]{1,0:T(2,128)S(1)}, u32[]{:S(2)}, u32[]{:S(2)}) %collective-permute-start.4) | collective-permute-done | bytes 393248 | tf_op jit(solution)/shard_map/ppermute | solution.py:101
  104.6 32.9 %all_gather.21 = f32[2,49152]{1,0:T(2,128)} all-gather(f32[2,6144]{1,0:T(2,128)S(1)} %copy-done.5), channel_id=1, replica_groups=mesh['cls'=4,'org'=8] {'org'}, dimensions={1}, use_global_device_ids=true | all-gather | bytes 442368 | tf_op jit(solution)/shard_map/all_gather | solution.py:87
  138.2 3.7 multiply_add_fusion
  143.3 15.2 %all_gather.25 = f32[49152]{0:T(1024)} all-gather(f32[6144]{0:T(1024)S(1)} %copy-done.7), channel_id=1, replica_groups=mesh['cls'=4,'org'=8] {'org'}, dimensions={0}, use_global_device_ids=true | all-gather | bytes 221184 | tf_op jit(solution)/shard_map/all_gather | solution.py:86
  158.4 14.6 %all_gather.22 = f32[2,49152]{1,0:T(2,128)S(1)} all-gather(f32[2,6144]{1,0:T(2,128)S(1)} %copy-done.6), channel_id=1, replica_groups=mesh['cls'=4,'org'=8] {'org'}, dimensions={1}, use_global_device_ids=true | all-gather | bytes 442368 | tf_op jit(solution)/shard_map/all_gather | solution.py:85
  174.5 2.6 reshape.94
  177.0 22.5 %all-gather.10.cloned.1.call-done = f32[4,2,49152]{2,1,0:T(2,128)} async-done(((f32[1,2,49152]{2,1,0:T(2,128)}), f32[4,2,49152]{2,1,0:T(2,128)}) %all-gather.10.cloned.1.call-update) | async-done | bytes 1572880 | tf_op jit(solution)/shard_map/all_gather | solution.py:91
  199.5 2.5 reshape.92
  202.0 30.2 %all-gather.14.cloned.1.call-done = f32[4,2,49152]{2,1,0:T(2,128)} async-done(((f32[1,2,49152]{2,1,0:T(2,128)}), f32[4,2,49152]{2,1,0:T(2,128)}) %all-gather.14.cloned.1.call-update) | async-done | bytes 1572880 | tf_op jit(solution)/shard_map/all_gather | solution.py:91
  232.2 3.6 reshape.96
  235.9 36.1 %all-gather.8.cloned.1.call-done = f32[2,8,49152]{2,1,0:T(8,128)} async-done(((f32[2,8,6144]{2,1,0:T(8,128)}), f32[2,8,49152]{2,1,0:T(8,128)}) %all-gather.8.cloned.1.call-update) | async-done | bytes 3145744 | tf_op jit(solution)/shard_map/all_gather | solution.py:84
  271.9 6.9 %multiply_reduce_fusion.1 = (f32[49152,2]{0,1:T(2,128)S(1)}, f32[49152,2]{0,1:T(2,128)S(1)}, f32[49152,2]{0,1:T(2,128)}) fusion(f32[2,8,49152]{2,1,0:T(8,128)} %all-gather.8.cloned.1.call-done, f32[49152,8]{0,1:T(8,128)S(1)} %bitcast.155, f32[49152,8]{0,1:T(8,128)} %bitcast.157, f32[49152,8]{0,1:T(8,128)S(1)} %bitcast.156), kind=kLoop, calls=%fused_computation.59 | loop fusion | flops 4423680 | bytes 9043968 | tf_op jit(solution)/shard_map/cel,el->cl/dot_general | solution.py:19
  281.1 39.4 %while.44 = (s32[]{:T(128)}, f32[2,1,60]{2,0,1:T(2,128)S(1)}, s32[8]{0:T(128)S(1)}, f32[2,49152]{1,0:T(2,128)S(1)}, s32[2,1,2,49152]{3,0,2,1:T(2,128)}, /*index=5*/s32[]{:T(128)}, s32[1]{0:T(128)}, s32[]{:T(128)}, s32[]{:T(128)}) while((s32[]{:T(128)}, f32[2,1,60]{2,0,1:T(2,128)S(1)}, s32[8]{0:T(128)S(1)}, ...), condition=%wide.region_6.7_spmd.clone, body=%wide.region_4.6_spmd.clone.sunk | while | flops 6943207 | bytes 3615725 | solution.py:62
  283.5 1.7 fusion.87
  288.5 1.7 fusion.87
  293.4 1.7 fusion.87
  298.3 1.7 fusion.87
  303.2 1.7 fusion.87
  308.2 1.7 fusion.87
  313.1 1.7 fusion.87
  318.0 1.7 fusion.87
  321.9 39.4 %while.45 = (s32[]{:T(128)}, f32[2,1,60]{2,0,1:T(2,128)S(1)}, s32[8]{0:T(128)S(1)}, f32[2,49152]{1,0:T(2,128)S(1)}, s32[2,1,2,49152]{3,0,2,1:T(2,128)}, /*index=5*/s32[]{:T(128)}, s32[1]{0:T(128)}, s32[]{:T(128)}, s32[]{:T(128)}) while((s32[]{:T(128)}, f32[2,1,60]{2,0,1:T(2,128)S(1)}, s32[8]{0:T(128)S(1)}, ...), condition=%wide.region_9.10_spmd.clone, body=%wide.region_7.9_spmd.clone.sunk | while | flops 6943207 | bytes 3615725 | solution.py:62
  324.4 1.7 fusion.93
  339.2 1.7 fusion.93
  344.1 1.7 fusion.93
  358.9 1.7 fusion.93
  361.9 39.6 %all-reduce = (f32[]{:T(128)}, f32[]{:T(128)}, f32[]{:T(128)}, f32[]{:T(128)}) all-reduce(f32[]{:T(128)} %fusion.53, f32[]{:T(128)} %get-tuple-element.186, f32[]{:T(128)} %fusion.54, f32[]{:T(128)} %get-tuple-element.185), channel_id=1, replica_groups=mesh['cls'=4,'org'=8] {'cls','org'}, use_global_device_ids=true, to_apply=%region_15.16 | all-reduce | flops 4 | bytes 32 | tf_op jit(solution)/shard_map/psum | solution.py:69
  (338 shorter events, 88.7 us)
Async XLA Ops:
  7.2 1.5 copy-start.9
  7.2 167.3 %all-gather.12.cloned.1.call-start = ((), (), s32[]{:S(2)}) async-start(), calls=%async_computation.2 | async-start | bytes 1966080 | tf_op jit(solution)/shard_map/all_gather | solution.py:91
  42.4 1.0 copy-start.1
  42.4 33.8 %collective-permute-start = (f32[2,49152]{1,0:T(2,128)S(1)}, f32[2,49152]{1,0:T(2,128)S(1)}, u32[]{:S(2)}, u32[]{:S(2)}) collective-permute-start(f32[2,49152]{1,0:T(2,128)S(1)} %bitcast.163), channel_id=1, source_target_pairs={{0,1},{1,0},{2,3},{3,2},{4,5},{5,4},{6,7},{7,6},{8,9},{9,8},{10,11... | collective-permute-start | bytes 1179656 | tf_op jit(solution)/shard_map/ppermute | solution.py:101
  75.6 13.6 %copy-start = (s32[2,1,2,49152]{3,0,2,1:T(2,128)}, s32[2,1,2,49152]{3,0,2,1:T(2,128)S(1)}, u32[]{:S(2)}) copy-start(s32[2,1,2,49152]{3,0,2,1:T(2,128)S(1)} %get-tuple-element.489) | copy-start | bytes 2359300
  75.7 3.4 collective-permute-start.3
  76.4 28.1 %copy-start.5 = (f32[2,6144]{1,0:T(2,128)S(1)}, f32[2,6144]{1,0:T(2,128)}, u32[]{:S(2)}) copy-start(f32[2,6144]{1,0:T(2,128)} %param.15) | copy-start | bytes 147460
  76.4 12.6 %collective-permute-start.1 = (f32[2,49152]{1,0:T(2,128)S(1)}, f32[2,49152]{1,0:T(2,128)S(1)}, u32[]{:S(2)}, u32[]{:S(2)}) collective-permute-start(f32[2,49152]{1,0:T(2,128)S(1)} %add.79), channel_id=1, source_target_pairs={{0,2},{1,3},{2,0},{3,1},{4,6},{5,7},{6,4},{7,5},{8,10},{9,11},{10,... | collective-permute-start | bytes 1179656 | tf_op jit(solution)/shard_map/ppermute | solution.py:101
  79.3 58.3 %copy-start.8 = (f32[2]{0:T(128)S(1)}, f32[2]{0:T(128)}, u32[]{:S(2)}) copy-start(f32[2]{0:T(128)} %param.21) | copy-start | bytes 28
  79.3 25.0 %collective-permute-start.4 = (f32[2,49152]{1,0:T(2,128)S(1)}, f32[2,49152]{1,0:T(2,128)S(1)}, u32[]{:S(2)}, u32[]{:S(2)}) collective-permute-start(f32[2,49152]{1,0:T(2,128)S(1)} %add.83), channel_id=1, source_target_pairs={{0,2},{1,3},{2,0},{3,1},{4,6},{5,7},{6,4},{7,5},{8,10},{9,11},{10,... | collective-permute-start | bytes 1179656 | tf_op jit(solution)/shard_map/ppermute | solution.py:101
  89.3 48.9 %collective-permute-start.2 = (f32[2,49152]{1,0:T(2,128)S(1)}, f32[2,49152]{1,0:T(2,128)S(1)}, u32[]{:S(2)}, u32[]{:S(2)}) collective-permute-start(f32[2,49152]{1,0:T(2,128)S(1)} %add.80), channel_id=1, source_target_pairs={{0,4},{1,5},{2,6},{3,7},{4,0},{5,1},{6,2},{7,3},{8,12},{9,13},{10,... | collective-permute-start | bytes 1179656 | tf_op jit(solution)/shard_map/ppermute | solution.py:101
  104.5 33.7 %collective-permute-start.5 = (f32[2,49152]{1,0:T(2,128)S(1)}, f32[2,49152]{1,0:T(2,128)S(1)}, u32[]{:S(2)}, u32[]{:S(2)}) collective-permute-start(f32[2,49152]{1,0:T(2,128)S(1)} %add.84), channel_id=1, source_target_pairs={{0,4},{1,5},{2,6},{3,7},{4,0},{5,1},{6,2},{7,3},{8,12},{9,13},{10,... | collective-permute-start | bytes 1179656 | tf_op jit(solution)/shard_map/ppermute | solution.py:101
  137.5 62.0 %all-gather.10.cloned.1.call-start = ((), (), s32[]{:S(2)}) async-start(), calls=%async_computation.1 | async-start | bytes 1966080 | tf_op jit(solution)/shard_map/all_gather | solution.py:91
  138.2 5.1 %copy-start.7 = (f32[6144]{0:T(1024)S(1)}, f32[6144]{0:T(1024)}, u32[]{:S(2)}) copy-start(f32[6144]{0:T(1024)} %param.18) | copy-start | bytes 73732
  138.2 20.2 %copy-start.6 = (f32[2,6144]{1,0:T(2,128)S(1)}, f32[2,6144]{1,0:T(2,128)}, u32[]{:S(2)}) copy-start(f32[2,6144]{1,0:T(2,128)} %param.17) | copy-start | bytes 147460
  141.9 90.3 %all-gather.14.cloned.1.call-start = ((), (), s32[]{:S(2)}) async-start(), calls=%async_computation.3 | async-start | bytes 1966080 | tf_op jit(solution)/shard_map/all_gather | solution.py:91
  142.7 129.3 %all-gather.8.cloned.1.call-start = ((), (), s32[]{:S(2)}) async-start(), calls=%async_computation | async-start | bytes 3538944 | tf_op jit(solution)/shard_map/all_gather | solution.py:84
  271.9 6.9 %copy-start.2 = (f32[49152]{0:T(1024)S(1)}, f32[49152]{0:T(1024)}, u32[]{:S(2)}) copy-start(f32[49152]{0:T(1024)} %all_gather.25) | copy-start | bytes 589828
  321.9 83.5 %copy-start.3 = (f32[49152]{0:T(1024)S(1)}, f32[49152]{0:T(1024)}, u32[]{:S(2)}) copy-start(f32[49152]{0:T(1024)} %all_gather.25) | copy-start | bytes 589828
  321.9 83.5 %copy-start.4 = (f32[49152,2]{0,1:T(2,128)S(1)}, f32[49152,2]{0,1:T(2,128)}, u32[]{:S(2)}) copy-start(f32[49152,2]{0,1:T(2,128)} %get-tuple-element.184) | copy-start | bytes 1179652
Sparse Core Ops, SparseCore 0:
  137.7 29.1 all-gather.11
  168.6 30.8 all-gather.9
  201.4 30.8 all-gather.13
  233.7 38.1 all-gather.7
